TPU v7x, 8 devices: a whole 2x2x1 slice. The times are simulated.
8 devices in a mesh: t: 4 (over z, y, x), v: 2 (over core).
Axes of the slice: x: 2, y: 2, z: 1, core: 2. Of those that a mesh axis runs over, the one named last changes fastest.
Arguments:
- hidden_in: bfloat16 [512, 2560], replicated
- seq_lens: int32 [512], replicated
- target: int32 [512], replicated
- g_attn_pre: bfloat16 [2560], replicated
- w_q: bfloat16 [2560, 2048], P(None, 't')
- w_k: bfloat16 [2560, 1024], P(None, 't')
- w_v: bfloat16 [2560, 1024], P(None, 't')
- w_o: bfloat16 [2048, 2560], P('t')
- g_attn_post: bfloat16 [2560], replicated
- g_mlp_pre: bfloat16 [2560], replicated
- w_gate: bfloat16 [2560, 10240], P(None, 't')
- w_up: bfloat16 [2560, 10240], P(None, 't')
- w_down: bfloat16 [10240, 2560], P('t')
- g_mlp_post: bfloat16 [2560], replicated
- g_final: bfloat16 [2560], replicated
- k_cache: bfloat16 [512, 32, 4, 256], P(None, None, 't')
- v_cache: bfloat16 [512, 32, 4, 256], P(None, None, 't')
- embed_table: bfloat16 [262144, 2560], P(('v', 't'))
Outputs:
- output 1: float32 [512], replicated
- output 2: bfloat16 [512, 2560], replicated
All inputs are finite; a program needn't handle non-finite values.
Results may differ from a plain program's by a relative error of at most 0.00777438.
Values sent between devices are 32-bit elements.
A program may use at most 1 GiB of HBM per device.

v0:
```python
import jax
import jax.numpy as jnp
from jax import lax
from jax.sharding import PartitionSpec as P

ATTN_CAP = 50.0
FINAL_CAP = 30.0
NORM_EPS = 1e-6
ROPE_BASE = 10000.0


def rms_norm(values, gain_vec):
    x_f32 = values.astype(jnp.float32)
    scaled = x_f32 * lax.rsqrt(jnp.mean(x_f32 * x_f32, axis=-1, keepdims=True) + NORM_EPS)
    return scaled * (1.0 + gain_vec.astype(jnp.float32))


def rotary(values, positions):
    half_dim = values.shape[-1] // 2
    inv_freq = ROPE_BASE ** (-2.0 * jnp.arange(half_dim, dtype=jnp.float32) / values.shape[-1])
    angles = positions.astype(jnp.float32)[:, None] * inv_freq[None, :]
    angles = angles.reshape((values.shape[0],) + (1,) * (values.ndim - 2) + (half_dim,))
    cos_t = jnp.cos(angles)
    sin_t = jnp.sin(angles)
    x_low = values[..., :half_dim]
    x_high = values[..., half_dim:]
    return jnp.concatenate([x_low * cos_t - x_high * sin_t, x_high * cos_t + x_low * sin_t], axis=-1)


def attention(normed, seq_lens, w_q, w_k, w_v, k_cache, v_cache):
    tokens, ctx_len, kv_heads, head_dim = k_cache.shape
    group_size = w_q.shape[1] // (kv_heads * head_dim)
    score_scale = head_dim ** -0.5
    q_rot = rotary(jnp.dot(normed, w_q, preferred_element_type=jnp.float32).reshape(tokens, kv_heads, group_size, head_dim), seq_lens).astype(jnp.bfloat16)
    k_rot = rotary(jnp.dot(normed, w_k, preferred_element_type=jnp.float32).reshape(tokens, kv_heads, head_dim), seq_lens).astype(jnp.bfloat16)
    v_new = jnp.dot(normed, w_v, preferred_element_type=jnp.float32).astype(jnp.bfloat16).reshape(tokens, kv_heads, head_dim)
    s_cache = jnp.einsum('nkgd,ntkd->nkgt', q_rot, k_cache, preferred_element_type=jnp.float32) * score_scale
    s_new = jnp.einsum('nkgd,nkd->nkg', q_rot, k_rot, preferred_element_type=jnp.float32) * score_scale
    s_cache = ATTN_CAP * jnp.tanh(s_cache / ATTN_CAP)
    s_new = ATTN_CAP * jnp.tanh(s_new / ATTN_CAP)
    valid_mask = jnp.arange(ctx_len)[None, :] < seq_lens[:, None]
    s_cache = jnp.where(valid_mask[:, None, None, :], s_cache, -1e30)
    row_max = jnp.maximum(jnp.max(s_cache, axis=-1), s_new)
    p_cache = jnp.exp(s_cache - row_max[..., None])
    p_new = jnp.exp(s_new - row_max)
    denominator = jnp.sum(p_cache, axis=-1) + p_new
    weighted = jnp.einsum('nkgt,ntkd->nkgd', p_cache.astype(jnp.bfloat16), v_cache, preferred_element_type=jnp.float32)
    weighted = weighted + p_new.astype(jnp.bfloat16).astype(jnp.float32)[..., None] * v_new.astype(jnp.float32)[:, :, None, :]
    return (weighted / denominator[..., None]).astype(jnp.bfloat16).reshape(tokens, kv_heads * group_size * head_dim)


def solution(mesh):
    tp_size = mesh.shape['t']
    in_specs = (P(), P(), P(), P(), P(None, 't'), P(None, 't'), P(None, 't'), P('t', None), P(), P(), P(None, 't'), P(None, 't'), P('t', None), P(), P(), P(None, None, 't', None), P(None, None, 't', None), P(('v', 't'), None))

    def local_step(hidden_in, seq_lens, target, g_attn_pre, w_q, w_k, w_v, w_o, g_attn_post, g_mlp_pre, w_gate, w_up, w_down, g_mlp_post, g_final, k_cache, v_cache, embed_table):
        normed = rms_norm(hidden_in, g_attn_pre).astype(jnp.bfloat16)
        attn_vec = attention(normed, seq_lens, w_q, w_k, w_v, k_cache, v_cache)
        attn_part = jnp.dot(attn_vec, w_o, preferred_element_type=jnp.float32)
        attn_out = lax.psum(attn_part, 't')
        hidden_mid = (hidden_in.astype(jnp.float32) + rms_norm(attn_out, g_attn_post)).astype(jnp.bfloat16)
        mlp_in = rms_norm(hidden_mid, g_mlp_pre).astype(jnp.bfloat16)
        gate_proj = jnp.dot(mlp_in, w_gate, preferred_element_type=jnp.float32)
        up_proj = jnp.dot(mlp_in, w_up, preferred_element_type=jnp.float32)
        activated = (jax.nn.gelu(gate_proj, approximate=True) * up_proj).astype(jnp.bfloat16)
        mlp_part = jnp.dot(activated, w_down, preferred_element_type=jnp.float32)
        mlp_out = lax.psum(mlp_part, 't')
        hidden_out = (hidden_mid.astype(jnp.float32) + rms_norm(mlp_out, g_mlp_post)).astype(jnp.bfloat16)
        final_h = rms_norm(hidden_out, g_final).astype(jnp.bfloat16)
        logits = lax.dot_general(final_h, embed_table, (((1,), (1,)), ((), ())), preferred_element_type=jnp.float32)
        capped = FINAL_CAP * jnp.tanh(logits / FINAL_CAP)
        vocab_local = embed_table.shape[0]
        shard_index = lax.axis_index('v') * tp_size + lax.axis_index('t')
        row_ids = shard_index * vocab_local + jnp.arange(vocab_local)
        local_max = jnp.max(capped, axis=1)
        local_sum = jnp.sum(jnp.exp(capped - local_max[:, None]), axis=1)
        local_tgt = jnp.sum(jnp.where(row_ids[None, :] == target[:, None], capped, 0.0), axis=1)
        gathered = lax.all_gather(jnp.stack([local_max, local_sum, local_tgt]), ('v', 't'))
        glob_max = jnp.max(gathered[:, 0], axis=0)
        glob_sum = jnp.sum(gathered[:, 1] * jnp.exp(gathered[:, 0] - glob_max[None, :]), axis=0)
        logprob = jnp.sum(gathered[:, 2], axis=0) - glob_max - jnp.log(glob_sum)
        return logprob, hidden_out

    return jax.shard_map(local_step, mesh=mesh, in_specs=in_specs, out_specs=(P(), P()), check_vma=False)
```

profile of v0, /device:TPU:0, one launch (start us, length us, event | category | flops | bytes accessed | tf_op | source)
XLA Modules:
  0.0 470.5 jit_solution(3995644555311958377)
XLA Ops:
  7.2 0.0 all-reduce.3.cloned.1.call-start
  7.2 0.8 convert_element_type.83
  8.1 0.8 iota_compare_fusion
  8.9 0.7 convert_add_fusion.6
  9.6 2.3 fusion.7
  11.9 4.2 fusion.81
  16.1 0.9 fusion.85
  17.0 2.1 copy.46
  19.1 1.0 copy.47
  20.1 3.2 convolution_bitcast_fusion
  23.3 1.9 multiply_cosine_fusion.1
  25.2 1.2 fusion.69
  26.4 0.9 maximum_convert_fusion
  27.2 1.2 copy.49
  28.5 1.8 fusion.66
  30.3 0.7 copy-done.4
  31.0 0.1 copy-done.5
  31.1 0.8 multiply_reduce_fusion.2
  31.8 0.1 copy.44
  32.0 6.7 %fusion.86 = (f32[512,2]{1,0:T(8,128)S(1)}, f32[512,2,32]{2,1,0:T(2,128)}) fusion(bf16[512,32,1,256]{3,1,2,0:T(8,128)(2,1)} %param.33, bf16[512,2,128]{2,1,0:T(2,128)(2,1)} %copy-done.5, bf16[512,2,128]{2,1,0:T(2,128)(2,1)} %copy-done.4, pred[512,32]{1,0:T(8,128)(4,1)S(1)} %iota_compare_fusion), kind=kOutput, calls=%fused_computation.110 | convolution fusion | flops 17955840 | bytes 9064448 | tf_op jit(solution)/shard_map/nkgd,ntkd->nkgt/dot_general | solution.py:37
  38.6 0.1 copy.34
  38.8 0.1 copy.35
  38.9 2.5 fusion.58
  41.5 0.1 copy.37
  41.6 0.9 copy.36
  42.5 0.8 copy.38
  43.3 3.1 fusion.27
  46.4 4.6 fusion.34
  51.1 0.1 copy.50
  51.2 3.9 fusion.88
  55.1 0.0 all-reduce.5.cloned.1.call-start
  55.2 112.1 %all-reduce.3.cloned.1.call-done = f32[512,2560]{1,0:T(8,128)} async-done(((f32[512,2560]{1,0:T(8,128)}), f32[512,2560]{1,0:T(8,128)}) %all-reduce.3.cloned.1.call-update) | async-done | bytes 5242896 | tf_op jit(solution)/shard_map/psum | solution.py:60
  167.3 3.1 multiply_reduce_fusion.1
  170.4 1.0 copy-done.3
  171.4 3.0 fusion.11
  174.4 11.7 %fusion.52 = f32[512,2560]{1,0:T(8,128)} fusion(bf16[2560,2560]{1,0:T(8,128)(2,1)} %param.28, bf16[512,2560]{1,0:T(8,128)(2,1)S(1)} %get-tuple-element.9, f32[2560]{0:T(1024)S(1)} %convert_add_fusion.4, f32[512]{0:T(512)S(1)} %add_rsqrt_fusion.2), kind=kOutput, calls=%fused_computation.52 | convolution fusion | flops 6716129280 | bytes 20983808 | tf_op jit(solution)/shard_map/dot_general | solution.py:63
  186.1 26.6 %fusion.49 = f32[512,2560]{1,0:T(8,128)} fusion(bf16[2560,2560]{1,0:T(8,128)(2,1)} %param.30, f32[512,2560]{1,0:T(8,128)} %fusion.52, bf16[2560,2560]{1,0:T(8,128)(2,1)} %param.29, bf16[512,2560]{1,0:T(8,128)(2,1)S(1)} %get-tuple-element.9, f32[2560]{0:T(1024)S(1)} %convert_add_fusion.4, f32[512]{0:T(512)S(1)} %add_rsqrt_fusion.2), kind=kOutput, calls=%fused_computation.51 | convolution fusion | flops 13440122880 | bytes 39333888 | tf_op jit(solution)/shard_map/dot_general | solution.py:66
  212.8 0.7 copy-done.12
  213.4 0.7 iota_add_fusion
  214.1 108.0 %all-reduce.5.cloned.1.call-done = f32[512,2560]{1,0:T(8,128)} async-done(((f32[512,2560]{1,0:T(8,128)}), f32[512,2560]{1,0:T(8,128)}) %all-reduce.5.cloned.1.call-update) | async-done | bytes 5242896 | tf_op jit(solution)/shard_map/psum | solution.py:67
  322.1 3.1 multiply_reduce_fusion
  325.2 1.0 copy-done.2
  326.2 2.7 fusion.4
  328.9 98.7 %fusion.87 = (f32[512]{0:T(512)S(1)}, f32[512,32768]{1,0:T(8,128)}) fusion(bf16[32768,2560]{1,0:T(8,128)(2,1)} %param.35, bf16[512,2560]{1,0:T(8,128)(2,1)} %get-tuple-element.7, f32[2560]{0:T(1024)S(1)} %convert_add_fusion.2, f32[512]{0:T(512)S(1)} %add_rsqrt_fusion), kind=kOutput, calls=%fused_computation.111 | convolution fusion | flops 85954920448 | bytes 237516800 | tf_op jit(solution)/shard_map/dot_general | solution.py:70
  427.7 24.3 %exponential_reduce_fusion = (f32[512]{0:T(512)S(1)}, f32[512]{0:T(512)S(1)}) fusion(f32[512,32768]{1,0:T(8,128)} %get-tuple-element.25, f32[512]{0:T(512)S(1)} %get-tuple-element.24, s32[512]{0:T(512)S(1)} %copy-done.14, s32[32768]{0:T(1024)S(1)} %copy-done.6), kind=kLoop, calls=%fused_computation.1 | loop fusion | flops 83885056 | bytes 67248128 | tf_op jit(solution)/shard_map/reduce_sum | solution.py:76
  451.9 11.0 %all-gather.1 = f32[8,3,512]{2,1,0:T(4,128)S(1)} all-gather(f32[1,3,512]{2,1,0:T(4,128)S(1)} %maximum_bitcast_fusion), channel_id=2, replica_groups=mesh['t'=4,'v'=2] {'v','t'}, dimensions={0}, use_global_device_ids=true | all-gather | bytes 55296 | tf_op jit(solution)/shard_map/all_gather | solution.py:78
  463.0 0.1 slice_reduce_fusion
  463.1 0.6 log_subtract_fusion
  (41 shorter events, 0.3 us)
Async XLA Ops:
  7.2 44.0 %copy-start = (bf16[512,2560]{1,0:T(8,128)(2,1)S(1)}, bf16[512,2560]{1,0:T(8,128)(2,1)}, u32[]{:S(2)}) copy-start(bf16[512,2560]{1,0:T(8,128)(2,1)} %param.25) | copy-start | bytes 7864324
  7.2 160.2 %all-reduce.3.cloned.1.call-start = ((), (), s32[]{:S(2)}) async-start(), calls=%async_computation | async-start | bytes 10485760 | tf_op jit(solution)/shard_map/psum | solution.py:60
  30.3 0.7 copy-start.4
  30.3 0.8 copy-start.5
  41.6 4.8 %copy-start.7 = (f32[512,2,32]{2,1,0:T(2,128)S(1)}, f32[512,2,32]{2,1,0:T(2,128)}, u32[]{:S(2)}) copy-start(f32[512,2,32]{2,1,0:T(2,128)} %get-tuple-element.23) | copy-start | bytes 393220
  43.3 3.1 copy-start.8
  43.3 3.1 copy-start.9
  51.2 4.0 copy-start.10
  51.2 4.0 copy-start.11
  55.1 267.0 %all-reduce.5.cloned.1.call-start = ((), (), s32[]{:S(2)}) async-start(), calls=%async_computation.1 | async-start | bytes 10485760 | tf_op jit(solution)/shard_map/psum | solution.py:67
  167.3 4.0 copy-start.3
  212.7 0.7 copy-start.12
  212.7 0.7 copy-start.13
  322.1 4.0 copy-start.2
  328.9 98.7 %copy-start.6 = (s32[32768]{0:T(1024)S(1)}, s32[32768]{0:T(1024)}, u32[]{:S(2)}) copy-start(s32[32768]{0:T(1024)} %iota_add_fusion) | copy-start | bytes 393220
  328.9 98.7 %copy-start.14 = (s32[512]{0:T(512)S(1)}, s32[512]{0:T(512)}, u32[]{:S(2)}) copy-start(s32[512]{0:T(512)} %param.20) | copy-start | bytes 6148
  427.7 36.0 %copy-start.1 = (bf16[512,2560]{1,0:T(8,128)(2,1)S(1)}, bf16[512,2560]{1,0:T(8,128)(2,1)}, u32[]{:S(2)}) copy-start(bf16[512,2560]{1,0:T(8,128)(2,1)} %param.25) | copy-start | bytes 7864324
Sparse Core Ops, SparseCore 0:
  55.2 112.0 all-reduce.2
  212.9 109.2 all-reduce.4
where the time goes:
time: 471 us
  waiting for transfers between devices  220 us (47%)
  matrix products  163 us (35%)
  other arithmetic  51.4 us (11%)
  between operations  14.3 us (3%)
  blocking collectives  11 us (2%)
  local copies, waits for them, and re-layouts  10.9 us (2%)
    psum x1, waiting for transfers between devices, local_step(): attn_out = lax.psum(attn_part, 't')  112 us
    psum x1, waiting for transfers between devices, local_step(): mlp_out = lax.psum(mlp_part, 't')  108 us
    dot_general x1, matrix products, local_step(): lax.dot_general(final_h, embed_table, (((1,), (1,)), ((), ())), preferred...  98.7 us
    dot_general x1, matrix products, local_step(): mlp_part = jnp.dot(activated, w_down, preferred_element_type=jnp.float32)  26.6 us
    reduce_sum x1, other arithmetic, local_step(): local_sum = jnp.sum(jnp.exp(capped - local_max[:, None]), axis=1)  24.3 us
    reduce_sum x5, other arithmetic, rms_norm(): jnp.mean(x_f32 * x_f32, axis=-1, keepdims=True) + NORM_EPS  14.2 us
    dot_general x1, matrix products, local_step(): gate_proj = jnp.dot(mlp_in, w_gate, preferred_element_type=jnp.float32)  11.7 us
    all_gather x1, blocking collectives, local_step(): lax.all_gather(jnp.stack([local_max, local_sum, local_tgt]), ('v', 't'))  11 us
  transfers between devices with their start and end apart: 2, of which 2 were waited for; matrix products, arithmetic and copies ran while one was open for 0% of the time, Pallas kernels for 0%

commit v1 on v0

--- a/solution.py
+++ b/solution.py
@@ -1,6 +1,8 @@
 import jax
 import jax.numpy as jnp
 from jax import lax
+from jax.experimental import pallas as pl
+from jax.experimental.pallas import tpu as pltpu
 from jax.sharding import PartitionSpec as P
 
 ATTN_CAP = 50.0
@@ -49,11 +51,66 @@
     return (weighted / denominator[..., None]).astype(jnp.bfloat16).reshape(tokens, kv_heads * group_size * head_dim)
 
 
+HEAD_ROWS = 2048
+HEAD_SUB = 256
+
+
+def head_kernel(base_ref, h_ref, tgt_ref, table_ref, sum_ref, hit_ref):
+    step = pl.program_id(0)
+
+    @pl.when(step == 0)
+    def _():
+        sum_ref[...] = jnp.zeros_like(sum_ref)
+        hit_ref[...] = jnp.zeros_like(hit_ref)
+
+    total = sum_ref[...]
+    hit = hit_ref[...]
+    target = tgt_ref[...] - (base_ref[0] + step * HEAD_ROWS)
+    tokens = total.shape[1]
+    for part in range(HEAD_ROWS // HEAD_SUB):
+        rows = table_ref[part * HEAD_SUB:(part + 1) * HEAD_SUB, :]
+        logits = jnp.dot(rows, h_ref[...], preferred_element_type=jnp.float32)
+        capped = FINAL_CAP * jnp.tanh(logits / FINAL_CAP)
+        row_ids = lax.broadcasted_iota(jnp.int32, logits.shape, 0) + part * HEAD_SUB
+        total = total + jnp.sum(jnp.exp(capped).reshape(HEAD_SUB // 8, 8, tokens), axis=0)
+        picked = jnp.where(row_ids == target, capped, 0.0)
+        hit = hit + jnp.sum(picked.reshape(HEAD_SUB // 8, 8, tokens), axis=0)
+    sum_ref[...] = total
+    hit_ref[...] = hit
+
+
+def head_sums(base, h_cols, target, table):
+    width, tokens = h_cols.shape
+    vocab = table.shape[0]
+    return pl.pallas_call(
+        head_kernel,
+        grid=(vocab // HEAD_ROWS,),
+        in_specs=[
+            pl.BlockSpec(memory_space=pltpu.SMEM),
+            pl.BlockSpec((width, tokens), lambda i: (0, 0)),
+            pl.BlockSpec((1, tokens), lambda i: (0, 0)),
+            pl.BlockSpec((HEAD_ROWS, width), lambda i: (i, 0)),
+        ],
+        out_specs=[pl.BlockSpec((8, tokens), lambda i: (0, 0))] * 2,
+        out_shape=[jax.ShapeDtypeStruct((8, tokens), jnp.float32)] * 2,
+        compiler_params=pltpu.CompilerParams(vmem_limit_bytes=56 * 2**20),
+        name='head_sums',
+    )(base, h_cols, target, table)
+
+
 def solution(mesh):
     tp_size = mesh.shape['t']
     in_specs = (P(), P(), P(), P(), P(None, 't'), P(None, 't'), P(None, 't'), P('t', None), P(), P(), P(None, 't'), P(None, 't'), P('t', None), P(), P(), P(None, None, 't', None), P(None, None, 't', None), P(('v', 't'), None))
 
     def local_step(hidden_in, seq_lens, target, g_attn_pre, w_q, w_k, w_v, w_o, g_attn_post, g_mlp_pre, w_gate, w_up, w_down, g_mlp_post, g_final, k_cache, v_cache, embed_table):
+        half = hidden_in.shape[0] // 2
+        core = lax.axis_index('v')
+        first = core * half
+        all_tokens = hidden_in
+        hidden_in = lax.dynamic_slice_in_dim(all_tokens, first, half, 0)
+        seq_lens = lax.dynamic_slice_in_dim(seq_lens, first, half, 0)
+        k_cache = lax.dynamic_slice_in_dim(k_cache, first, half, 0)
+        v_cache = lax.dynamic_slice_in_dim(v_cache, first, half, 0)
         normed = rms_norm(hidden_in, g_attn_pre).astype(jnp.bfloat16)
         attn_vec = attention(normed, seq_lens, w_q, w_k, w_v, k_cache, v_cache)
         attn_part = jnp.dot(attn_vec, w_o, preferred_element_type=jnp.float32)
@@ -65,20 +122,17 @@
         activated = (jax.nn.gelu(gate_proj, approximate=True) * up_proj).astype(jnp.bfloat16)
         mlp_part = jnp.dot(activated, w_down, preferred_element_type=jnp.float32)
         mlp_out = lax.psum(mlp_part, 't')
-        hidden_out = (hidden_mid.astype(jnp.float32) + rms_norm(mlp_out, g_mlp_post)).astype(jnp.bfloat16)
-        final_h = rms_norm(hidden_out, g_final).astype(jnp.bfloat16)
-        logits = lax.dot_general(final_h, embed_table, (((1,), (1,)), ((), ())), preferred_element_type=jnp.float32)
-        capped = FINAL_CAP * jnp.tanh(logits / FINAL_CAP)
+        half_out = (hidden_mid.astype(jnp.float32) + rms_norm(mlp_out, g_mlp_post)).astype(jnp.bfloat16)
+        full_out = lax.all_gather(half_out.astype(jnp.float32), 'v', tiled=True)
+        final_h = rms_norm(full_out, g_final).astype(jnp.bfloat16)
+        hidden_out = full_out.astype(jnp.bfloat16)
         vocab_local = embed_table.shape[0]
-        shard_index = lax.axis_index('v') * tp_size + lax.axis_index('t')
-        row_ids = shard_index * vocab_local + jnp.arange(vocab_local)
-        local_max = jnp.max(capped, axis=1)
-        local_sum = jnp.sum(jnp.exp(capped - local_max[:, None]), axis=1)
-        local_tgt = jnp.sum(jnp.where(row_ids[None, :] == target[:, None], capped, 0.0), axis=1)
-        gathered = lax.all_gather(jnp.stack([local_max, local_sum, local_tgt]), ('v', 't'))
-        glob_max = jnp.max(gathered[:, 0], axis=0)
-        glob_sum = jnp.sum(gathered[:, 1] * jnp.exp(gathered[:, 0] - glob_max[None, :]), axis=0)
-        logprob = jnp.sum(gathered[:, 2], axis=0) - glob_max - jnp.log(glob_sum)
+        shard_index = core * tp_size + lax.axis_index('t')
+        base = (shard_index * vocab_local).astype(jnp.int32).reshape(1)
+        local_sum, local_hit = head_sums(base, final_h.T, target[None, :], embed_table)
+        stats = jnp.stack([jnp.sum(local_sum, axis=0), jnp.sum(local_hit, axis=0)])
+        stats = lax.psum(stats, ('v', 't'))
+        logprob = stats[1] - jnp.log(stats[0])
         return logprob, hidden_out
 
     return jax.shard_map(local_step, mesh=mesh, in_specs=in_specs, out_specs=(P(), P()), check_vma=False)

time: 471 us -> 357 us (0.76)
  matrix products: 163 us -> 41.8 us
  Pallas kernels: 0 us -> 100 us
  waiting for transfers between devices: 220 us -> 147 us
  other arithmetic: 51.4 us -> 19.4 us
  blocking collectives: 11 us -> 23.3 us
    pallas_call x0 -> x1, Pallas kernels: none -> 100 us  [head_sums(): pl.pallas_call(head_kernel, grid=(vocab // HEAD_ROWS,), in_specs=[pl.Bloc...]
    dot_general x1 -> x0, matrix products: 98.7 us -> none  [local_step(): lax.dot_general(final_h, embed_table, (((1,), (1,)), ((), ())), preferred...]
    psum x1, waiting for transfers between devices: 112 us -> 68.9 us  [local_step(): attn_out = lax.psum(attn_part, 't')]
    psum x1, waiting for transfers between devices: 108 us -> 66 us  [local_step(): mlp_out = lax.psum(mlp_part, 't')]
    psum x0 -> x1, blocking collectives: none -> 23.3 us  [local_step(): stats = lax.psum(stats, ('v', 't'))]
    reduce_sum x3 -> x2, other arithmetic: 24.3 us -> 1.47 us  [local_step(): stats = jnp.stack([jnp.sum(local_sum, axis=0), jnp.sum(local_hit, axis=0)])]
    all_gather x0 -> x1, waiting for transfers between devices: none -> 12.4 us  [local_step(): full_out = lax.all_gather(half_out.astype(jnp.float32), 'v', tiled=True)]
    all_gather x1 -> x0, blocking collectives: 11 us -> none  [local_step(): lax.all_gather(jnp.stack([local_max, local_sum, local_tgt]), ('v', 't'))]
  transfers between devices with their start and end apart: 2 -> 3, of which waited for: 2 -> 3; matrix products, arithmetic and copies ran while one was open for 0% -> 0% of each run, Pallas kernels for 0% -> 0%
where the time goes in v1:
time: 357 us; the launch traced here: 356 us
  waiting for transfers between devices  147 us (41%)
  Pallas kernels  100 us (28%)
  matrix products  41.8 us (12%)
  blocking collectives  23.3 us (7%)
  other arithmetic  19.4 us (5%)
  between operations  14 us (4%)
  local copies, waits for them, and re-layouts  9.71 us (3%)
    pallas_call x1, Pallas kernels, head_sums(): pl.pallas_call(head_kernel, grid=(vocab // HEAD_ROWS,), in_specs=[pl.Bloc...  100 us
    psum x1, waiting for transfers between devices, local_step(): attn_out = lax.psum(attn_part, 't')  68.9 us
    psum x1, waiting for transfers between devices, local_step(): mlp_out = lax.psum(mlp_part, 't')  66 us
    psum x1, blocking collectives, local_step(): stats = lax.psum(stats, ('v', 't'))  23.3 us
    dot_general x1, matrix products, local_step(): mlp_part = jnp.dot(activated, w_down, preferred_element_type=jnp.float32)  15.9 us
    all_gather x1, waiting for transfers between devices, local_step(): full_out = lax.all_gather(half_out.astype(jnp.float32), 'v', tiled=True)  12.4 us
    dot_general x1, matrix products, local_step(): gate_proj = jnp.dot(mlp_in, w_gate, preferred_element_type=jnp.float32)  9.87 us
    reduce_sum x5, other arithmetic, rms_norm(): jnp.mean(x_f32 * x_f32, axis=-1, keepdims=True) + NORM_EPS  8.57 us
  transfers between devices with their start and end apart: 3, of which 3 were waited for; matrix products, arithmetic and copies ran while one was open for 0% of the time, Pallas kernels for 0%

profile of v1, /device:TPU:0, one launch (start us, length us, event | category | flops | bytes accessed | tf_op | source)
XLA Modules:
  0.0 356.2 jit_solution(13460721223747707369)
XLA Ops:
  7.2 0.8 convert_add_fusion.6
  8.1 0.8 fusion.81
  8.9 0.1 iota_compare_fusion
  9.0 1.1 constant_dynamic-slice_fusion
  10.1 1.6 copy.47
  11.7 0.4 fusion.7
  12.1 0.5 multiply_cosine_fusion.1
  12.6 2.3 convolution_bitcast_fusion
  14.9 0.6 fusion.66
  15.5 0.1 copy.48
  15.7 2.5 fusion.39
  18.2 1.7 fusion.78
  19.8 0.3 reshape.309
  20.2 0.3 fusion.63
  20.5 0.4 multiply_reduce_fusion.3
  21.0 3.5 fusion.83
  24.4 0.1 copy.32
  24.5 0.1 copy.33
  24.7 0.7 fusion.55
  25.5 0.1 copy.34
  25.7 0.1 copy.36
  25.8 3.5 fusion.43
  29.3 2.6 fusion.84
  32.0 0.2 all-reduce.5.cloned.1.call-start
  32.2 0.4 copy-done.6
  32.7 68.9 %all-reduce.3.cloned.1.call-done = f32[256,2560]{0,1:T(8,128)} async-done(((f32[256,2560]{0,1:T(8,128)}), f32[256,2560]{0,1:T(8,128)}) %all-reduce.3.cloned.1.call-update) | async-done | bytes 2621456 | tf_op jit(solution)/shard_map/psum | solution.py:117
  101.6 2.2 multiply_reduce_fusion.2
  103.8 0.3 copy-done.3
  104.1 0.7 fusion.11
  104.8 9.9 %fusion.49 = f32[256,2560]{1,0:T(8,128)} fusion(bf16[2560,2560]{1,0:T(8,128)(2,1)} %param.28, bf16[256,2560]{0,1:T(8,128)(2,1)S(1)} %get-tuple-element.13, f32[2560]{0:T(1024)S(1)} %convert_add_fusion.4, f32[256]{0:T(256)S(1)} %add_rsqrt_fusion.2), kind=kOutput, calls=%fused_computation.48 | convolution fusion | flops 3358064640 | bytes 17050624 | tf_op jit(solution)/shard_map/dot_general | solution.py:120
  114.7 15.9 %fusion.46 = f32[256,2560]{0,1:T(8,128)} fusion(bf16[2560,2560]{1,0:T(8,128)(2,1)} %param.30, bf16[2560,2560]{1,0:T(8,128)(2,1)} %param.29, f32[256,2560]{1,0:T(8,128)} %fusion.49, bf16[256,2560]{0,1:T(8,128)(2,1)S(1)} %get-tuple-element.13, f32[2560]{0:T(1024)S(1)} %convert_add_fusion.4, f32[256]{0:T(256)S(1)} %add_rsqrt_fusion.2), kind=kOutput, calls=%fused_computation.46 | convolution fusion | flops 6720061440 | bytes 32779264 | tf_op jit(solution)/shard_map/dot_general | solution.py:123
  130.6 0.3 all-gather.2.cloned.1.call-start
  130.9 0.4 copy-done.8
  131.3 66.0 %all-reduce.5.cloned.1.call-done = f32[256,2560]{0,1:T(8,128)} async-done(((f32[256,2560]{0,1:T(8,128)}), f32[256,2560]{0,1:T(8,128)}) %all-reduce.5.cloned.1.call-update) | async-done | bytes 2621456 | tf_op jit(solution)/shard_map/psum | solution.py:124
  197.3 2.2 multiply_reduce_fusion.1
  199.6 0.3 copy-done.4
  199.8 2.0 fusion.23
  201.8 0.7 copy-done.9
  202.5 12.4 %all-gather.2.cloned.1.call-done = f32[512,2560]{0,1:T(8,128)} async-done(((f32[256,2560]{0,1:T(8,128)}), f32[512,2560]{0,1:T(8,128)}) %all-gather.2.cloned.1.call-update) | async-done | bytes 5242896 | tf_op jit(solution)/shard_map/all_gather | solution.py:126
  214.9 3.0 multiply_reduce_fusion
  218.0 1.0 copy-done.2
  218.9 2.5 fusion.82
  221.4 2.8 copy.39
  224.2 100.0 %head_sums.1 = (f32[8,512]{1,0:T(8,128)}, f32[8,512]{1,0:T(8,128)}) custom-call(s32[1]{0:T(128)} %bitcast.1.base_ref, bf16[2560,512]{1,0:T(8,128)(2,1)} %get-tuple-element.17.h_ref, s32[1,512]{1,0:T(1,128)} %bitcast.56, bf16[32768,2560]{1,0:T(8,128)(2,1)} %table_ref.1), custom_call_target="tpu_custom_call" | custom-call | tf_op jit(solution)/shard_map/head_sums/pallas_call | solution.py:85
  324.2 0.7 reduce_sum.78
  325.0 0.7 reduce_sum.79
  325.7 23.3 %psum.23 = f32[2,512]{1,0:T(2,128)S(1)} all-reduce(f32[2,512]{1,0:T(2,128)S(1)} %pad_maximum_fusion.1), channel_id=1, replica_groups=mesh['t'=4,'v'=2] {'v','t'}, use_global_device_ids=true, to_apply=%region_11.12 | all-reduce | flops 1024 | bytes 8192 | tf_op jit(solution)/shard_map/psum | solution.py:134
  349.0 0.6 fusion.67
  (37 shorter events, 0.5 us)
Async XLA Ops:
  7.2 1.8 copy-start
  7.2 94.4 %all-reduce.3.cloned.1.call-start = ((), (), s32[]{:S(2)}) async-start(), calls=%async_computation | async-start | bytes 5242880 | tf_op jit(solution)/shard_map/psum | solution.py:117
  15.7 2.5 copy-start.10
  25.8 3.5 copy-start.5
  32.0 0.7 copy-start.6
  32.0 0.7 copy-start.7
  32.0 165.3 %all-reduce.5.cloned.1.call-start = ((), (), s32[]{:S(2)}) async-start(), calls=%async_computation.1 | async-start | bytes 5242880 | tf_op jit(solution)/shard_map/psum | solution.py:124
  101.6 2.5 copy-start.3
  130.6 0.7 copy-start.8
  130.6 84.3 %all-gather.2.cloned.1.call-start = ((), (), s32[]{:S(2)}) async-start(), calls=%async_computation.2 | async-start | bytes 7864320 | tf_op jit(solution)/shard_map/all_gather | solution.py:126
  197.3 2.5 copy-start.4
  201.8 0.7 copy-start.9
  214.9 4.0 %copy-start.2 = (f32[512,2560]{0,1:T(8,128)S(1)}, f32[512,2560]{0,1:T(8,128)}, u32[]{:S(2)}) copy-start(f32[512,2560]{0,1:T(8,128)} %all-gather.2.cloned.1.call-done) | copy-start | bytes 15728644
  224.2 125.4 %copy-start.1 = (bf16[512,2560]{1,0:T(8,128)(2,1)S(1)}, bf16[512,2560]{1,0:T(8,128)(2,1)}, u32[]{:S(2)}) copy-start(bf16[512,2560]{1,0:T(8,128)(2,1)} %param.18) | copy-start | bytes 7864324
Sparse Core Ops, SparseCore 0:
  32.1 69.4 all-reduce.2
  130.7 66.5 all-reduce.4
  201.9 12.9 all-gather.1

commit v2 on v0

v2 whole, which is shorter than its diff:
```python
import jax
import jax.numpy as jnp
from jax import lax
from jax.experimental import pallas as pl
from jax.experimental.pallas import tpu as pltpu
from jax.sharding import PartitionSpec as P

ATTN_CAP = 50.0
FINAL_CAP = 30.0
NORM_EPS = 1e-6
ROPE_BASE = 10000.0


def rms_norm(values, gain_vec):
    x_f32 = values.astype(jnp.float32)
    scaled = x_f32 * lax.rsqrt(jnp.mean(x_f32 * x_f32, axis=-1, keepdims=True) + NORM_EPS)
    return scaled * (1.0 + gain_vec.astype(jnp.float32))


def rotary(values, positions):
    half_dim = values.shape[-1] // 2
    inv_freq = ROPE_BASE ** (-2.0 * jnp.arange(half_dim, dtype=jnp.float32) / values.shape[-1])
    angles = positions.astype(jnp.float32)[:, None] * inv_freq[None, :]
    angles = angles.reshape((values.shape[0],) + (1,) * (values.ndim - 2) + (half_dim,))
    cos_t = jnp.cos(angles)
    sin_t = jnp.sin(angles)
    x_low = values[..., :half_dim]
    x_high = values[..., half_dim:]
    return jnp.concatenate([x_low * cos_t - x_high * sin_t, x_high * cos_t + x_low * sin_t], axis=-1)


def attention(normed, seq_lens, w_q, w_k, w_v, k_cache, v_cache):
    tokens, ctx_len, kv_heads, head_dim = k_cache.shape
    group_size = w_q.shape[1] // (kv_heads * head_dim)
    score_scale = head_dim ** -0.5
    q_rot = rotary(jnp.dot(normed, w_q, preferred_element_type=jnp.float32).reshape(tokens, kv_heads, group_size, head_dim), seq_lens).astype(jnp.bfloat16)
    k_rot = rotary(jnp.dot(normed, w_k, preferred_element_type=jnp.float32).reshape(tokens, kv_heads, head_dim), seq_lens).astype(jnp.bfloat16)
    v_new = jnp.dot(normed, w_v, preferred_element_type=jnp.float32).astype(jnp.bfloat16).reshape(tokens, kv_heads, head_dim)
    s_cache = jnp.einsum('nkgd,ntkd->nkgt', q_rot, k_cache, preferred_element_type=jnp.float32) * score_scale
    s_new = jnp.einsum('nkgd,nkd->nkg', q_rot, k_rot, preferred_element_type=jnp.float32) * score_scale
    s_cache = ATTN_CAP * jnp.tanh(s_cache / ATTN_CAP)
    s_new = ATTN_CAP * jnp.tanh(s_new / ATTN_CAP)
    valid_mask = jnp.arange(ctx_len)[None, :] < seq_lens[:, None]
    s_cache = jnp.where(valid_mask[:, None, None, :], s_cache, -1e30)
    row_max = jnp.maximum(jnp.max(s_cache, axis=-1), s_new)
    p_cache = jnp.exp(s_cache - row_max[..., None])
    p_new = jnp.exp(s_new - row_max)
    denominator = jnp.sum(p_cache, axis=-1) + p_new
    weighted = jnp.einsum('nkgt,ntkd->nkgd', p_cache.astype(jnp.bfloat16), v_cache, preferred_element_type=jnp.float32)
    weighted = weighted + p_new.astype(jnp.bfloat16).astype(jnp.float32)[..., None] * v_new.astype(jnp.float32)[:, :, None, :]
    return (weighted / denominator[..., None]).astype(jnp.bfloat16).reshape(tokens, kv_heads * group_size * head_dim)


FIRST_GROUPS = 11
MESH = pl.DeviceIdType.MESH
BLOCK = 16
TILE = 512
SLOTS = 15
GROUP = 4
SUB = 256
CHUNKS = 2


def norm_rows(values, gain):
    return values * lax.rsqrt(jnp.mean(values * values, axis=-1, keepdims=True) + NORM_EPS) * (1.0 + gain)


def layer_head_kernel(
    part_hbm, x_hbm, tgt_ref, g_attn_ref, g_pre_ref, g_post_ref, g_final_ref, wg, wu, wd, table,
    logprob_ref, y_hbm,
    ring, part, landed, gat, oth, h, stage, act, mlp_in, xown, x1, zbuf, acc_sum, acc_hit, stats, stats_in,
    load_sem, part_sem, x_sem, y_sem, send_sem, recv_sem, pair_send, pair_recv, stat_send, stat_recv,
):
    t = lax.axis_index('t')
    v = lax.axis_index('v')
    x, y = lax.rem(t, 2), lax.div(t, 2)
    to_x = {'t': t + 1 - 2 * x}
    to_y = {'t': t + 2 - 4 * y}
    to_pair = {'v': 1 - v}
    half = part.shape[0]
    rows = half // CHUNKS
    vocab = table.shape[0]
    tiles = vocab // TILE
    base = (v * 4 + t) * vocab

    def b1(c, xo, yo):
        return c * rows + (xo * 2 + yo) * BLOCK

    def b2(c, yo, xo):
        return c * rows + rows // 2 + (yo * 2 + xo) * BLOCK

    def at(ref, row):
        return ref.at[pl.ds(pl.multiple_of(row, BLOCK), BLOCK), :]

    def remote(src, dst, send, recv, device):
        return pltpu.make_async_remote_copy(src_ref=src, dst_ref=dst, send_sem=send, recv_sem=recv, device_id=device, device_id_type=MESH)

    def weight_loads():
        out = []
        for n, w in enumerate((wg, wu, wd)):
            for k in range(5):
                slot = n * 5 + k
                out.append(pltpu.make_async_copy(w.at[pl.ds(k * TILE, TILE), :], ring.at[pl.ds(slot * TILE, TILE), :], load_sem.at[slot]))
        return out

    def table_load(q):
        slot = lax.rem(q, SLOTS)
        row = pl.multiple_of(lax.rem(q, tiles) * TILE, TILE)
        return pltpu.make_async_copy(table.at[pl.ds(row, TILE), :], ring.at[pl.ds(pl.multiple_of(slot * TILE, TILE), TILE), :], load_sem.at[slot])

    def scatter_copies(c, phase):
        s, r = send_sem.at[phase, c], recv_sem.at[phase, c]
        return (
            remote(at(part, b1(c, 1 - x, 1 - y)), landed.at[c, 0], s.at[0], r.at[0], to_x),
            remote(at(part, b1(c, 1 - x, y)), landed.at[c, 1], s.at[1], r.at[1], to_x),
            remote(at(part, b1(c, x, 1 - y)), landed.at[c, 2], s.at[2], r.at[2], to_y),
            remote(at(part, b2(c, 1 - y, 1 - x)), landed.at[c, 3], s.at[3], r.at[3], to_y),
            remote(at(part, b2(c, 1 - y, x)), landed.at[c, 4], s.at[4], r.at[4], to_y),
            remote(at(part, b2(c, y, 1 - x)), landed.at[c, 5], s.at[5], r.at[5], to_x),
        )

    def gather_copies(c, phase):
        s, r = send_sem.at[phase, c], recv_sem.at[phase, c]

        def same(row, k, device):
            return remote(at(gat, row), at(gat, row), s.at[k], r.at[k], device)

        return (
            same(b1(c, x, y), 0, to_y),
            same(b1(c, x, y), 1, to_x),
            same(b1(c, x, 1 - y), 2, to_x),
            same(b2(c, y, x), 3, to_x),
            same(b2(c, y, x), 4, to_y),
            same(b2(c, y, 1 - x), 5, to_y),
        )

    def scatter_start(c, phase):
        copies = scatter_copies(c, phase)
        for k in (0, 3, 1, 4):
            copies[k].start()

    def scatter_forward(c, phase):
        copies = scatter_copies(c, phase)
        for k, row in ((0, b1(c, x, 1 - y)), (3, b2(c, y, 1 - x))):
            copies[k].wait_recv()
            dst = at(part, row)
            dst[...] = dst[...] + landed[c, k]
            copies[k + 2].start()

    def scatter_finish_gather_start(c, phase):
        copies = scatter_copies(c, phase)
        out = gather_copies(c, phase + 1)
        for side, (k, row) in enumerate(((0, b1(c, x, y)), (3, b2(c, y, x)))):
            copies[k + 1].wait_recv()
            copies[k + 2].wait_recv()
            total = at(part, row)[...] + landed[c, k + 1] + landed[c, k + 2]
            mine = c * 2 + side
            if phase == 0:
                if c == 0 and side == 0:
                    for i in range(2 * CHUNKS):
                        own_x(i).wait()
                mid = (xown[mine].astype(jnp.float32) + norm_rows(total, g_attn_ref[...])).astype(jnp.bfloat16)
                x1[mine] = mid
                value = norm_rows(mid.astype(jnp.float32), g_pre_ref[...])
            else:
                value = x1[mine].astype(jnp.float32) + norm_rows(total, g_post_ref[...])
            at(gat, row)[...] = value.astype(jnp.bfloat16).astype(jnp.float32)
            out[k].start()
            out[k + 1].start()

    def gather_forward(c, phase):
        copies = gather_copies(c, phase)
        for k in (0, 3):
            copies[k].wait_recv()
            copies[k + 2].start()

    def gather_finish(c, phase):
        copies = gather_copies(c, phase)
        for k in (1, 2, 4, 5):
            copies[k].wait_recv()

    def drain(c, phase):
        for copy in scatter_copies(c, phase) + gather_copies(c, phase + 1):
            copy.wait_send()

    def own_x(i):
        c, side = i // 2, i % 2
        row = (b1(c, x, y), b2(c, y, x))[side] + v * half
        return pltpu.make_async_copy(at(x_hbm, row), xown.at[i], x_sem.at[i])

    def mlp(c, last):
        loads = weight_loads()
        mlp_in[...] = gat[c * rows:(c + 1) * rows, :].astype(jnp.bfloat16)
        for k in range(10):
            loads[k].wait()

        def gate_up(n, carry):
            cols = pl.ds(pl.multiple_of(n * TILE, TILE), TILE)
            gate = jnp.dot(mlp_in[...], ring[0:2560, cols], preferred_element_type=jnp.float32)
            up = jnp.dot(mlp_in[...], ring[2560:5120, cols], preferred_element_type=jnp.float32)
            act[:, cols] = (jax.nn.gelu(gate, approximate=True) * up).astype(jnp.bfloat16)
            return carry

        lax.fori_loop(0, 5, gate_up, 0)
        for k in range(10):
            if last:
                table_load(k).start()
            else:
                loads[k].start()
        for k in range(10, 15):
            loads[k].wait()
        drain(c, 0)

        def down(n, carry):
            cols = pl.ds(pl.multiple_of(n * TILE, TILE), TILE)
            part[c * rows:(c + 1) * rows, cols] = jnp.dot(act[...], ring[5120:7680, cols], preferred_element_type=jnp.float32)
            return carry

        lax.fori_loop(0, 5, down, 0)
        for k in range(10, 15):
            if last:
                table_load(k).start()
            else:
                loads[k].start()

    def pair_copy(c):
        span = pl.ds(c * rows, rows)
        return remote(gat.at[span, :], oth.at[span, :], pair_send.at[c], pair_recv.at[c], to_pair)

    def y_copies(c):
        out = []
        for k, owner in enumerate((v, 1 - v)):
            dst = y_hbm.at[pl.ds(pl.multiple_of(owner * half + c * rows, BLOCK), rows), :]
            out.append(pltpu.make_async_copy(stage.at[pl.ds(k * rows, rows), :], dst, y_sem.at[c, k]))
        return out

    def final_norm(c):
        pair = pair_copy(c)
        if c > 0:
            for copy in y_copies(c - 1):
                copy.wait()
        for k, (src, owner) in enumerate(((gat, v), (oth, 1 - v))):
            if k == 1:
                pair.wait_recv()

            def body(i, carry):
                row = pl.multiple_of(i * BLOCK, BLOCK)
                value = src[pl.ds(c * rows + row, BLOCK), :]
                stage[pl.ds(k * rows + row, BLOCK), :] = value.astype(jnp.bfloat16)
                h[pl.ds(pl.multiple_of((c * 2 + owner) * rows + row, BLOCK), BLOCK), :] = norm_rows(value, g_final_ref[...]).astype(jnp.bfloat16)
                return carry

            lax.fori_loop(0, rows // BLOCK, body, 0)
            y_copies(c)[k].start()

    def reduce_logits(logits, first_row, lo, width, keep):
        capped = FINAL_CAP * jnp.tanh(logits / FINAL_CAP)
        row_ids = lax.broadcasted_iota(jnp.int32, logits.shape, 0)
        wanted = tgt_ref[:, lo:lo + width] - (base + first_row)
        total = jnp.sum(jnp.exp(capped).reshape(SUB // 8, 8, width), axis=0)
        hit = jnp.sum(jnp.where(row_ids == wanted, capped, 0.0).reshape(SUB // 8, 8, width), axis=0)
        if keep is not None:
            total = jnp.where(keep, total, 0.0)
            hit = jnp.where(keep, hit, 0.0)
        acc_sum[:, lo:lo + width] += total
        acc_hit[:, lo:lo + width] += hit

    def head(first, last, lo, width, total_tiles, opens, closes):
        def body(g, carry):
            q0 = g * GROUP
            for k in range(GROUP):
                table_load(q0 + k).wait()
            pending = zbuf[:, 0:width]
            pending_row = lax.rem(q0, tiles) * TILE - SUB
            keep = g > first if opens else None
            for k in range(GROUP):
                slot = lax.rem(q0 + k, SLOTS)
                for j in range(TILE // SUB):
                    row = pl.multiple_of(slot * TILE + j * SUB, SUB)
                    logits = lax.dot_general(ring[pl.ds(row, SUB), :], h[lo:lo + width, :], (((1,), (1,)), ((), ())), preferred_element_type=jnp.float32)
                    reduce_logits(pending, pending_row, lo, width, keep)
                    keep = None
                    pending = logits
                    pending_row = lax.rem(q0 + k, tiles) * TILE + j * SUB
            zbuf[:, 0:width] = pending
            for k in range(GROUP):
                @pl.when(q0 + k + SLOTS < total_tiles)
                def _():
                    table_load(q0 + k + SLOTS).start()
            return carry

        lax.fori_loop(first, last, body, 0)
        if closes:
            reduce_logits(zbuf[:, 0:width], (last * GROUP % tiles or tiles) * TILE - SUB, lo, width, None)

    def stat_copy(r, device):
        return remote(stats.at[r], stats_in.at[r], stat_send.at[r], stat_recv.at[r], device)

    barrier = pltpu.get_barrier_semaphore()
    part_copy = pltpu.make_async_copy(part_hbm, part, part_sem)
    part_copy.start()
    for i in range(2 * CHUNKS):
        own_x(i).start()
    for copy in weight_loads():
        copy.start()
    for device in (to_x, to_y, to_pair):
        pl.semaphore_signal(barrier, inc=1, device_id=device, device_id_type=MESH)
    acc_sum[...] = jnp.zeros_like(acc_sum)
    acc_hit[...] = jnp.zeros_like(acc_hit)
    zbuf[...] = jnp.zeros_like(zbuf)
    stats[...] = jnp.zeros_like(stats)
    pl.semaphore_wait(barrier, 3)
    part_copy.wait()

    split = FIRST_GROUPS
    groups = tiles // GROUP
    total_tiles = tiles + split * GROUP
    scatter_start(0, 0)
    scatter_forward(0, 0)
    scatter_finish_gather_start(0, 0)
    gather_forward(0, 1)
    scatter_start(1, 0)
    gather_finish(0, 1)
    mlp(0, False)
    scatter_start(0, 2)
    scatter_forward(0, 2)
    scatter_forward(1, 0)
    scatter_finish_gather_start(0, 2)
    gather_forward(0, 3)
    scatter_finish_gather_start(1, 0)
    gather_finish(0, 3)
    pair_copy(0).start()
    gather_forward(1, 1)
    final_norm(0)
    gather_finish(1, 1)
    mlp(1, True)
    scatter_start(1, 2)
    head(0, 2, 0, 256, total_tiles, True, False)
    scatter_forward(1, 2)
    head(2, 4, 0, 256, total_tiles, False, False)
    scatter_finish_gather_start(1, 2)
    head(4, 6, 0, 256, total_tiles, False, False)
    gather_forward(1, 3)
    head(6, 8, 0, 256, total_tiles, False, False)
    gather_finish(1, 3)
    pair_copy(1).start()
    head(8, split, 0, 256, total_tiles, False, True)
    final_norm(1)
    head(split, groups, 0, 512, total_tiles, True, True)
    head(groups, groups + split, 256, 256, total_tiles, True, True)

    stats[0, 0:1, :] = jnp.sum(acc_sum[...], axis=0, keepdims=True)
    stats[0, 1:2, :] = jnp.sum(acc_hit[...], axis=0, keepdims=True)
    for r, device in enumerate((to_pair, to_x, to_y)):
        copy = stat_copy(r, device)
        copy.start()
        copy.wait_recv()
        if r < 2:
            stats[r + 1] = stats[r] + stats_in[r]
    both = stats[2] + stats_in[2]
    result = both[1:2, :] - jnp.log(both[0:1, :])
    for c in range(CHUNKS):
        for k in range(2):
            lo = (c * 2 + k) * rows
            logprob_ref[:, k * half + c * rows:k * half + (c + 1) * rows] = result[:, lo:lo + rows]

    for copy in y_copies(CHUNKS - 1):
        copy.wait()
    for r, device in enumerate((to_pair, to_x, to_y)):
        stat_copy(r, device).wait_send()
    for c in range(CHUNKS):
        drain(c, 2)
        pair_copy(c).wait_send()


def layer_head(part, x, target, g_attn_post, g_mlp_pre, g_mlp_post, g_final, w_gate, w_up, w_down, table):
    tokens, width = x.shape
    half = tokens // 2
    rows = half // CHUNKS
    f32, bf16 = jnp.float32, jnp.bfloat16
    vmem, dma = pltpu.VMEM, pltpu.SemaphoreType.DMA
    any_spec = pl.BlockSpec(memory_space=pl.ANY)
    vmem_spec = pl.BlockSpec(memory_space=pltpu.VMEM)
    gains = [g.astype(f32)[None, :] for g in (g_attn_post, g_mlp_pre, g_mlp_post, g_final)]
    ordered = target.reshape(2, CHUNKS, rows).transpose(1, 0, 2).reshape(1, tokens)
    logprob, hidden = pl.pallas_call(
        layer_head_kernel,
        in_specs=[any_spec, any_spec] + [vmem_spec] * 5 + [any_spec] * 4,
        out_specs=[vmem_spec, any_spec],
        out_shape=[jax.ShapeDtypeStruct((1, tokens), f32), jax.ShapeDtypeStruct((tokens, width), bf16)],
        scratch_shapes=[
            vmem((SLOTS * TILE, width), bf16),
            vmem((half, width), f32),
            vmem((CHUNKS, 6, BLOCK, width), f32),
            vmem((half, width), f32),
            vmem((half, width), f32),
            vmem((tokens, width), bf16),
            vmem((half, width), bf16),
            vmem((rows, width), bf16),
            vmem((rows, width), bf16),
            vmem((2 * CHUNKS, BLOCK, width), bf16),
            vmem((2 * CHUNKS, BLOCK, width), bf16),
            vmem((SUB, tokens), f32),
            vmem((8, tokens), f32),
            vmem((8, tokens), f32),
            vmem((3, 8, tokens), f32),
            vmem((3, 8, tokens), f32),
            dma((SLOTS,)),
            dma,
            dma((2 * CHUNKS,)),
            dma((CHUNKS, 2)),
            dma((4, CHUNKS, 6)),
            dma((4, CHUNKS, 6)),
            dma((CHUNKS,)),
            dma((CHUNKS,)),
            dma((3,)),
            dma((3,)),
        ],
        compiler_params=pltpu.CompilerParams(collective_id=0, has_side_effects=True, vmem_limit_bytes=66_500_000),
        name='layer_head',
    )(part, x, ordered, *gains, w_gate, w_up, w_down, table)
    return logprob.reshape(tokens), hidden


def solution(mesh):
    in_specs = (P(), P(), P(), P(), P(None, 't'), P(None, 't'), P(None, 't'), P('t', None), P(), P(), P(None, 't'), P(None, 't'), P('t', None), P(), P(), P(None, None, 't', None), P(None, None, 't', None), P(('v', 't'), None))

    def local_step(hidden_in, seq_lens, target, g_attn_pre, w_q, w_k, w_v, w_o, g_attn_post, g_mlp_pre, w_gate, w_up, w_down, g_mlp_post, g_final, k_cache, v_cache, embed_table):
        half = hidden_in.shape[0] // 2
        first = lax.axis_index('v') * half

        def mine(array):
            return lax.dynamic_slice_in_dim(array, first, half, 0)

        lens = mine(seq_lens)
        normed = rms_norm(mine(hidden_in), g_attn_pre).astype(jnp.bfloat16)
        attn_vec = attention(normed, lens, w_q, w_k, w_v, mine(k_cache), mine(v_cache))
        part = jnp.dot(attn_vec, w_o, preferred_element_type=jnp.float32)
        logprob, hidden_out = layer_head(part, hidden_in, target, g_attn_post, g_mlp_pre, g_mlp_post, g_final, w_gate, w_up, w_down, embed_table)
        return logprob, hidden_out

    return jax.shard_map(local_step, mesh=mesh, in_specs=in_specs, out_specs=(P(), P()), check_vma=False)
```

time: 471 us -> 239 us (0.51)
  waiting for transfers between devices: 220 us -> 0 us
  Pallas kernels: 0 us -> 202 us
  matrix products: 163 us -> 15.4 us
  other arithmetic: 51.4 us -> 7.96 us
  between operations: 14.3 us -> 0.81 us
  blocking collectives: 11 us -> 0 us
    psum x2 -> x0, waiting for transfers between devices: 220 us -> none  [the longest x1 112 us: local_step(): attn_out = lax.psum(attn_part, 't')]
    pallas_call x0 -> x1, Pallas kernels: none -> 202 us  [layer_head(): pl.pallas_call(layer_head_kernel, in_specs=[any_spec, any_spec] + [vmem_s...]
    dot_general x4 -> x1, matrix products: 141 us -> 2.34 us  [local_step(): part = jnp.dot(attn_vec, w_o, preferred_element_type=jnp.float32)]
    reduce_sum x3 -> x0, other arithmetic: 24.3 us -> none  [the longest x1 24.3 us: local_step(): local_sum = jnp.sum(jnp.exp(capped - local_max[:, None]), axis=1)]
    reduce_sum x5 -> x1, other arithmetic: 14.2 us -> 1.66 us  [rms_norm(): jnp.mean(x_f32 * x_f32, axis=-1, keepdims=True) + NORM_EPS]
    all_gather x1 -> x0, blocking collectives: 11 us -> none  [local_step(): lax.all_gather(jnp.stack([local_max, local_sum, local_tgt]), ('v', 't'))]
    broadcast_in_dim x0 -> x4, local copies, waits for them, and re-layouts: none -> 5.17 us  [layer_head(): g.astype(f32)[None, :]]
  transfers between devices with their start and end apart: 2 -> 0, of which waited for: 2 -> 0; matrix products, arithmetic and copies ran while one was open for 0% -> 0% of each run, Pallas kernels for 0% -> 0%
where the time goes in v2:
time: 239 us
  Pallas kernels  202 us (85%)
  matrix products  15.4 us (6%)
  local copies, waits for them, and re-layouts  12.3 us (5%)
  other arithmetic  7.96 us (3%)
    pallas_call x1, Pallas kernels, layer_head(): pl.pallas_call(layer_head_kernel, in_specs=[any_spec, any_spec] + [vmem_s...  202 us
    broadcast_in_dim x4, local copies, waits for them, and re-layouts, layer_head(): g.astype(f32)[None, :]  5.17 us
    unnamed x14, local copies, waits for them, and re-layouts  4.85 us

profile of v2, /device:TPU:0, one launch (start us, length us, event | category | flops | bytes accessed | tf_op | source)
XLA Modules:
  0.0 238.7 jit_solution(8904541318071447037)
XLA Ops:
  0.6 1.7 fusion.6
  2.3 1.3 copy.30
  3.6 0.8 fusion.55
  4.3 1.3 reshape.284.g_attn_ref
  5.6 1.3 reshape.285.g_pre_ref
  6.9 1.3 reshape.286.g_post_ref
  8.2 1.3 reshape.287.g_final_ref
  9.5 0.7 convert_add_fusion
  10.2 0.7 iota_compare_fusion
  10.9 0.0 copy-start
  10.9 2.6 %convolution_bitcast_fusion = f32[256,1,256]{0,2,1:T(8,128)S(1)} fusion(bf16[2560,256]{1,0:T(8,128)(2,1)} %param.23, f32[2560]{0:T(1024)S(1)} %convert_add_fusion, f32[256]{0:T(256)S(1)} %add_rsqrt_fusion, bf16[512,2560]{1,0:T(8,128)(2,1)} %x_hbm.1, s32[]{:T(128)S(6)} %select_n.11), kind=kOutput, calls=%fused_computation.15 | convolution fusion | flops 338165760 | bytes 2894852 | tf_op jit(solution)/shard_map/dot_general | solution.py:37
  13.5 0.6 fusion.46
  14.2 0.1 copy.36
  14.3 0.0 copy-start.3
  14.3 1.2 multiply_cosine_fusion.1
  15.5 0.0 copy-done
  15.5 2.6 %fusion.24 = f32[256,256]{1,0:T(8,128)} fusion(bf16[2560,256]{1,0:T(8,128)(2,1)} %param.24, f32[2560]{0:T(1024)S(1)} %convert_add_fusion, f32[256]{0:T(256)S(1)} %add_rsqrt_fusion, bf16[512,2560]{1,0:T(8,128)(2,1)S(1)} %copy-done, s32[]{:T(128)S(6)} %select_n.11), kind=kOutput, calls=%fused_computation.18 | convolution fusion | flops 338296832 | bytes 2896900 | tf_op jit(solution)/shard_map/dot_general | solution.py:38
  18.1 0.0 copy-done.3
  18.1 0.9 fusion.53
  19.0 0.0 copy-start.2
  19.0 0.3 reshape.276
  19.4 1.2 fusion.43
  20.5 0.4 multiply_reduce_fusion
  20.9 0.1 copy.35
  21.0 0.0 copy-done.2
  21.0 0.0 copy-start.4
  21.0 3.5 %fusion.56 = (f32[256,2]{1,0:T(8,128)S(1)}, f32[256,2,32]{2,1,0:T(2,128)S(1)}) fusion(bf16[512,32,1,256]{3,1,2,0:T(8,128)(2,1)} %param.33, s32[]{:T(128)S(6)} %select_n.11, bf16[256,2,128]{2,1,0:T(2,128)(2,1)S(1)} %get-tuple-element.9, bf16[256,2,128]{2,1,0:T(2,128)(2,1)S(1)} %get-tuple-element.8, pred[256,32]{1,0:T(8,128)(4,1)S(1)} %copy-done.2), kind=kOutput, calls=%fused_computation.59 | convolution fusion | flops 8977920 | bytes 4532228 | tf_op jit(solution)/shard_map/nkgd,ntkd->nkgt/dot_general | solution.py:39
  24.5 0.1 copy.25
  24.7 0.1 copy.26
  24.8 0.7 fusion.35
  25.5 0.1 copy.28
  25.6 0.1 copy.27
  25.8 0.1 copy.29
  25.9 0.0 copy-done.4
  25.9 0.0 copy-start.1
  26.0 3.4 %fusion.28 = bf16[256,2,256]{2,1,0:T(2,128)(2,1)S(1)} fusion(bf16[512,32,1,256]{3,1,2,0:T(8,128)(2,1)} %param.34, s32[]{:T(128)S(6)} %select_n.11, f32[256,2]{1,0:T(8,128)S(1)} %copy.29, f32[256,256]{1,0:T(8,128)S(1)} %copy-done.4, f32[256,2]{1,0:T(8,128)S(1)} %copy.27, f32[256,2,32]{2,1,0:T(2,128)S(1)} %get-tuple-element.17, f32[256,2]{1,0:T(8,128)S(1)} %copy.26), kind=kOutput, calls=%fused_computation.20 | convolution fusion | flops 8945664 | bytes 4790276 | tf_op jit(solution)/shard_map/nkgt,ntkd->nkgd/dot_general | solution.py:49
  29.4 0.0 copy-done.1
  29.4 2.3 fusion.57.part_hbm
  31.8 202.2 %layer_head.1 = (f32[1,512]{1,0:T(1,128)}, bf16[512,2560]{1,0:T(8,128)(2,1)}) custom-call(f32[256,2560]{1,0:T(8,128)} %fusion.57.part_hbm, bf16[512,2560]{1,0:T(8,128)(2,1)} %x_hbm.1, s32[1,512]{1,0:T(1,128)} %bitcast.48, f32[1,2560]{1,0:T(1,128)} %reshape.284.g_attn_ref, f32[1,2560]{1,0:T(1,128)} %reshape.285.g_pre_ref, f32[1,2560]{1,0:T(1,128)} %reshape.286.g_post_ref, ...), custom_call_target="tpu_custom_call" | custom-call | tf_op jit(solution)/shard_map/layer_head/pallas_call | solution.py:386
  234.0 1.3 copy.40
  235.3 3.4 %copy.41 = bf16[512,2560]{1,0:T(8,128)(2,1)} copy(bf16[512,2560]{1,0:T(8,128)(2,1)} %get-tuple-element.21) | data formatting | bytes 5242880
  (6 shorter events, 0.1 us)
Async XLA Ops:
  10.9 4.6 %copy-start = (bf16[512,2560]{1,0:T(8,128)(2,1)S(1)}, bf16[512,2560]{1,0:T(8,128)(2,1)}, u32[]{:S(2)}) copy-start(bf16[512,2560]{1,0:T(8,128)(2,1)} %x_hbm.1) | copy-start | bytes 7864324
  14.3 3.8 %copy-start.3 = (bf16[2560,512]{1,0:T(8,128)(2,1)S(1)}, bf16[2560,512]{1,0:T(8,128)(2,1)}, u32[]{:S(2)}) copy-start(bf16[2560,512]{1,0:T(8,128)(2,1)} %param.22) | copy-start | bytes 7864324
  19.0 2.0 copy-start.2
  21.0 4.9 %copy-start.4 = (f32[256,256]{1,0:T(8,128)S(1)}, f32[256,256]{1,0:T(8,128)}, u32[]{:S(2)}) copy-start(f32[256,256]{1,0:T(8,128)} %fusion.24) | copy-start | bytes 786436
  25.9 3.5 %copy-start.1 = (bf16[512,2560]{1,0:T(8,128)(2,1)S(1)}, bf16[512,2560]{1,0:T(8,128)(2,1)}, u32[]{:S(2)}) copy-start(bf16[512,2560]{1,0:T(8,128)(2,1)} %param.25) | copy-start | bytes 7864324

commit v3 on v2

--- a/solution.py
+++ b/solution.py
@@ -1,5 +1,6 @@
 import jax
 import jax.numpy as jnp
+import numpy as np
 from jax import lax
 from jax.experimental import pallas as pl
 from jax.experimental.pallas import tpu as pltpu
@@ -9,48 +10,8 @@
 FINAL_CAP = 30.0
 NORM_EPS = 1e-6
 ROPE_BASE = 10000.0
-
-
-def rms_norm(values, gain_vec):
-    x_f32 = values.astype(jnp.float32)
-    scaled = x_f32 * lax.rsqrt(jnp.mean(x_f32 * x_f32, axis=-1, keepdims=True) + NORM_EPS)
-    return scaled * (1.0 + gain_vec.astype(jnp.float32))
-
-
-def rotary(values, positions):
-    half_dim = values.shape[-1] // 2
-    inv_freq = ROPE_BASE ** (-2.0 * jnp.arange(half_dim, dtype=jnp.float32) / values.shape[-1])
-    angles = positions.astype(jnp.float32)[:, None] * inv_freq[None, :]
-    angles = angles.reshape((values.shape[0],) + (1,) * (values.ndim - 2) + (half_dim,))
-    cos_t = jnp.cos(angles)
-    sin_t = jnp.sin(angles)
-    x_low = values[..., :half_dim]
-    x_high = values[..., half_dim:]
-    return jnp.concatenate([x_low * cos_t - x_high * sin_t, x_high * cos_t + x_low * sin_t], axis=-1)
-
-
-def attention(normed, seq_lens, w_q, w_k, w_v, k_cache, v_cache):
-    tokens, ctx_len, kv_heads, head_dim = k_cache.shape
-    group_size = w_q.shape[1] // (kv_heads * head_dim)
-    score_scale = head_dim ** -0.5
-    q_rot = rotary(jnp.dot(normed, w_q, preferred_element_type=jnp.float32).reshape(tokens, kv_heads, group_size, head_dim), seq_lens).astype(jnp.bfloat16)
-    k_rot = rotary(jnp.dot(normed, w_k, preferred_element_type=jnp.float32).reshape(tokens, kv_heads, head_dim), seq_lens).astype(jnp.bfloat16)
-    v_new = jnp.dot(normed, w_v, preferred_element_type=jnp.float32).astype(jnp.bfloat16).reshape(tokens, kv_heads, head_dim)
-    s_cache = jnp.einsum('nkgd,ntkd->nkgt', q_rot, k_cache, preferred_element_type=jnp.float32) * score_scale
-    s_new = jnp.einsum('nkgd,nkd->nkg', q_rot, k_rot, preferred_element_type=jnp.float32) * score_scale
-    s_cache = ATTN_CAP * jnp.tanh(s_cache / ATTN_CAP)
-    s_new = ATTN_CAP * jnp.tanh(s_new / ATTN_CAP)
-    valid_mask = jnp.arange(ctx_len)[None, :] < seq_lens[:, None]
-    s_cache = jnp.where(valid_mask[:, None, None, :], s_cache, -1e30)
-    row_max = jnp.maximum(jnp.max(s_cache, axis=-1), s_new)
-    p_cache = jnp.exp(s_cache - row_max[..., None])
-    p_new = jnp.exp(s_new - row_max)
-    denominator = jnp.sum(p_cache, axis=-1) + p_new
-    weighted = jnp.einsum('nkgt,ntkd->nkgd', p_cache.astype(jnp.bfloat16), v_cache, preferred_element_type=jnp.float32)
-    weighted = weighted + p_new.astype(jnp.bfloat16).astype(jnp.float32)[..., None] * v_new.astype(jnp.float32)[:, :, None, :]
-    return (weighted / denominator[..., None]).astype(jnp.bfloat16).reshape(tokens, kv_heads * group_size * head_dim)
-
-
+CONTEXT = 32
+HEAD_DIM = 256
 FIRST_GROUPS = 11
 MESH = pl.DeviceIdType.MESH
 BLOCK = 16
@@ -66,10 +27,12 @@
 
 
 def layer_head_kernel(
-    part_hbm, x_hbm, tgt_ref, g_attn_ref, g_pre_ref, g_post_ref, g_final_ref, wg, wu, wd, table,
+    lens_in, tgt_in, freq_ref, g_first_in, g_attn_in, g_pre_in, g_post_in, g_final_in,
+    x_hbm, wq, wk, wv, wo, kc, vc, wg, wu, wd, table,
     logprob_ref, y_hbm,
-    ring, part, landed, gat, oth, h, stage, act, mlp_in, xown, x1, zbuf, acc_sum, acc_hit, stats, stats_in,
-    load_sem, part_sem, x_sem, y_sem, send_sem, recv_sem, pair_send, pair_recv, stat_send, stat_recv,
+    ring, part, landed, gat, oth, h, stage, work, x1, heads, trig, lens_ref, gains, tgt_ref,
+    zbuf, acc_sum, acc_hit, stats, stats_in,
+    load_sem, early_sem, y_sem, send_sem, recv_sem, pair_send, pair_recv, stat_send, stat_recv,
 ):
     t = lax.axis_index('t')
     v = lax.axis_index('v')
@@ -156,14 +119,11 @@
             total = at(part, row)[...] + landed[c, k + 1] + landed[c, k + 2]
             mine = c * 2 + side
             if phase == 0:
-                if c == 0 and side == 0:
-                    for i in range(2 * CHUNKS):
-                        own_x(i).wait()
-                mid = (xown[mine].astype(jnp.float32) + norm_rows(total, g_attn_ref[...])).astype(jnp.bfloat16)
+                mid = (at(stage, row)[...].astype(jnp.float32) + norm_rows(total, gains[1:2, :])).astype(jnp.bfloat16)
                 x1[mine] = mid
-                value = norm_rows(mid.astype(jnp.float32), g_pre_ref[...])
+                value = norm_rows(mid.astype(jnp.float32), gains[2:3, :])
             else:
-                value = x1[mine].astype(jnp.float32) + norm_rows(total, g_post_ref[...])
+                value = x1[mine].astype(jnp.float32) + norm_rows(total, gains[3:4, :])
             at(gat, row)[...] = value.astype(jnp.bfloat16).astype(jnp.float32)
             out[k].start()
             out[k + 1].start()
@@ -183,45 +143,137 @@
         for copy in scatter_copies(c, phase) + gather_copies(c, phase + 1):
             copy.wait_send()
 
-    def own_x(i):
-        c, side = i // 2, i % 2
-        row = (b1(c, x, y), b2(c, y, x))[side] + v * half
-        return pltpu.make_async_copy(at(x_hbm, row), xown.at[i], x_sem.at[i])
+    def early_loads():
+        local = v * half
+        pairs = [(x_hbm.at[pl.ds(pl.multiple_of(local, BLOCK), half), :], stage)]
+        col = 0
+        for w in (wq, wk, wv):
+            pairs.append((w, ring.at[pl.ds(5120, 2560), pl.ds(col, w.shape[1])]))
+            col += w.shape[1]
+        for cache, first in ((kc, 0), (vc, 4)):
+            for j in range(4):
+                row = pl.multiple_of((local + j * 64) * CONTEXT, 2048)
+                pairs.append((cache.at[pl.ds(row, 64 * CONTEXT), :], ring.at[pl.ds(2560, 64 * CONTEXT), pl.ds((first + j) * HEAD_DIM, HEAD_DIM)]))
+        pairs.append((wo, h))
+        return [pltpu.make_async_copy(src, dst, early_sem.at[i]) for i, (src, dst) in enumerate(pairs)]
+
+    def rotate(z, c):
+        low, high = z[:, 0:128], z[:, 128:256]
+        cos, sin = trig[0], trig[1]
+        return jnp.concatenate([low * cos - high * sin, high * cos + low * sin], axis=1)
+
+    def project():
+        early = early_loads()
+        early[0].wait()
+
+        def body(i, carry):
+            row = pl.multiple_of(i * BLOCK, BLOCK)
+            work[pl.ds(row, BLOCK), :] = norm_rows(stage[pl.ds(row, BLOCK), :].astype(jnp.float32), gains[0:1, :]).astype(jnp.bfloat16)
+            return carry
+
+        lax.fori_loop(0, half // BLOCK, body, 0)
+        for k in (1, 2, 3):
+            early[k].wait()
+        for n in range(4):
+            z = jnp.dot(work[...], ring[5120:7680, n * HEAD_DIM:(n + 1) * HEAD_DIM], preferred_element_type=jnp.float32)
+            if n < 3:
+                z = rotate(z, n)
+            heads[:, n * HEAD_DIM:(n + 1) * HEAD_DIM] = z.astype(jnp.bfloat16).astype(jnp.float32)
+
+    def attend(c):
+        early = early_loads()
+        for j in (2 * c, 2 * c + 1):
+            early[4 + j].wait()
+            early[8 + j].wait()
+        shape = (16, 8 * CONTEXT)
+        lane = lax.broadcasted_iota(jnp.int32, shape, 1)
+        same_token = lax.rem(lax.broadcasted_iota(jnp.int32, shape, 0), 8) == lax.div(lane, CONTEXT)
+        place = lax.rem(lane, CONTEXT).astype(jnp.float32)
+
+        def twice(a):
+            return jnp.concatenate([a, a], axis=0)
+
+        def body(j, carry):
+            k_cols = pl.ds(pl.multiple_of(j * HEAD_DIM, HEAD_DIM), HEAD_DIM)
+            v_cols = pl.ds(pl.multiple_of((j + 4) * HEAD_DIM, HEAD_DIM), HEAD_DIM)
+            for g in range(8):
+                row = pl.ds(pl.multiple_of(j * 64 + g * 8, 8), 8)
+                block = slice(2560 + g * 8 * CONTEXT, 2560 + (g + 1) * 8 * CONTEXT)
+                q = jnp.concatenate([heads[row, 0:256], heads[row, 256:512]], axis=0)
+                new_k = twice(heads[row, 512:768])
+                new_v = twice(heads[row, 768:1024])
+                length = twice(lens_ref[row, 0:1])
+                scores = lax.dot_general(q.astype(jnp.bfloat16), ring[block, k_cols], (((1,), (1,)), ((), ())), preferred_element_type=jnp.float32)
+                scores = ATTN_CAP * jnp.tanh(scores * HEAD_DIM ** -0.5 / ATTN_CAP)
+                fresh = jnp.sum(q * new_k, axis=1, keepdims=True)
+                fresh = ATTN_CAP * jnp.tanh(fresh * HEAD_DIM ** -0.5 / ATTN_CAP)
+                scores = jnp.where(same_token & (place < length), scores, -1e30)
+                top = jnp.maximum(jnp.max(scores, axis=1, keepdims=True), fresh)
+                weight = jnp.exp(scores - top)
+                fresh = jnp.exp(fresh - top)
+                norm = jnp.sum(weight, axis=1, keepdims=True) + fresh
+                mixed = jnp.dot(weight.astype(jnp.bfloat16), ring[block, v_cols], preferred_element_type=jnp.float32)
+                mixed = (mixed + fresh.astype(jnp.bfloat16).astype(jnp.float32) * new_v) / norm
+                heads[row, 0:256] = mixed[0:8, :]
+                heads[row, 256:512] = mixed[8:16, :]
+            return carry
+
+        lax.fori_loop(2 * c, 2 * c + 2, body, 0)
+        if c == 0:
+            early[12].wait()
+        vec = heads[c * rows:(c + 1) * rows, 0:512].astype(jnp.bfloat16)
+        for n in range(5):
+            cols = slice(n * TILE, (n + 1) * TILE)
+            part[c * rows:(c + 1) * rows, cols] = jnp.dot(vec, h[:, cols], preferred_element_type=jnp.float32)
+
+    def setup():
+        for i, g in enumerate((g_first_in, g_attn_in, g_pre_in, g_post_in, g_final_in)):
+            gains[i:i + 1, :] = g[...].astype(jnp.float32).reshape(1, g.shape[0])
+        for c in range(CHUNKS):
+            lens = jnp.where(v == 0, lens_in[c * rows:(c + 1) * rows], lens_in[half + c * rows:half + (c + 1) * rows])
+            column = jnp.broadcast_to(lens.astype(jnp.float32).reshape(1, rows), (rows, rows)).T
+            lens_ref[c * rows:(c + 1) * rows, :] = column
+            angle = column * freq_ref[...]
+            trig[0, c * rows:(c + 1) * rows, :] = jnp.cos(angle)
+            trig[1, c * rows:(c + 1) * rows, :] = jnp.sin(angle)
+            for k in range(2):
+                lo = (c * 2 + k) * rows
+                tgt_ref[:, lo:lo + rows] = tgt_in[k * half + c * rows:k * half + (c + 1) * rows].reshape(1, rows)
 
     def mlp(c, last):
         loads = weight_loads()
-        mlp_in[...] = gat[c * rows:(c + 1) * rows, :].astype(jnp.bfloat16)
+        work[0:rows, :] = gat[c * rows:(c + 1) * rows, :].astype(jnp.bfloat16)
         for k in range(10):
             loads[k].wait()
 
         def gate_up(n, carry):
             cols = pl.ds(pl.multiple_of(n * TILE, TILE), TILE)
-            gate = jnp.dot(mlp_in[...], ring[0:2560, cols], preferred_element_type=jnp.float32)
-            up = jnp.dot(mlp_in[...], ring[2560:5120, cols], preferred_element_type=jnp.float32)
-            act[:, cols] = (jax.nn.gelu(gate, approximate=True) * up).astype(jnp.bfloat16)
+            gate = jnp.dot(work[0:rows, :], ring[0:2560, cols], preferred_element_type=jnp.float32)
+            up = jnp.dot(work[0:rows, :], ring[2560:5120, cols], preferred_element_type=jnp.float32)
+            work[rows:2 * rows, cols] = (jax.nn.gelu(gate, approximate=True) * up).astype(jnp.bfloat16)
             return carry
 
         lax.fori_loop(0, 5, gate_up, 0)
         for k in range(10):
             if last:
-                table_load(k).start()
+                table_load(k).start(priority=1)
             else:
-                loads[k].start()
+                loads[k].start(priority=1)
         for k in range(10, 15):
             loads[k].wait()
         drain(c, 0)
 
         def down(n, carry):
             cols = pl.ds(pl.multiple_of(n * TILE, TILE), TILE)
-            part[c * rows:(c + 1) * rows, cols] = jnp.dot(act[...], ring[5120:7680, cols], preferred_element_type=jnp.float32)
+            part[c * rows:(c + 1) * rows, cols] = jnp.dot(work[rows:2 * rows, :], ring[5120:7680, cols], preferred_element_type=jnp.float32)
             return carry
 
         lax.fori_loop(0, 5, down, 0)
         for k in range(10, 15):
             if last:
-                table_load(k).start()
+                table_load(k).start(priority=1)
             else:
-                loads[k].start()
+                loads[k].start(priority=1)
 
     def pair_copy(c):
         span = pl.ds(c * rows, rows)
@@ -247,7 +299,7 @@
                 row = pl.multiple_of(i * BLOCK, BLOCK)
                 value = src[pl.ds(c * rows + row, BLOCK), :]
                 stage[pl.ds(k * rows + row, BLOCK), :] = value.astype(jnp.bfloat16)
-                h[pl.ds(pl.multiple_of((c * 2 + owner) * rows + row, BLOCK), BLOCK), :] = norm_rows(value, g_final_ref[...]).astype(jnp.bfloat16)
+                h[pl.ds(pl.multiple_of((c * 2 + owner) * rows + row, BLOCK), BLOCK), :] = norm_rows(value, gains[4:5, :]).astype(jnp.bfloat16)
                 return carry
 
             lax.fori_loop(0, rows // BLOCK, body, 0)
@@ -286,7 +338,7 @@
             for k in range(GROUP):
                 @pl.when(q0 + k + SLOTS < total_tiles)
                 def _():
-                    table_load(q0 + k + SLOTS).start()
+                    table_load(q0 + k + SLOTS).start(priority=1)
             return carry
 
         lax.fori_loop(first, last, body, 0)
@@ -297,25 +349,28 @@
         return remote(stats.at[r], stats_in.at[r], stat_send.at[r], stat_recv.at[r], device)
 
     barrier = pltpu.get_barrier_semaphore()
-    part_copy = pltpu.make_async_copy(part_hbm, part, part_sem)
-    part_copy.start()
-    for i in range(2 * CHUNKS):
-        own_x(i).start()
-    for copy in weight_loads():
+    for copy in early_loads():
         copy.start()
+    for copy in weight_loads()[0:5]:
+        copy.start(priority=1)
     for device in (to_x, to_y, to_pair):
         pl.semaphore_signal(barrier, inc=1, device_id=device, device_id_type=MESH)
     acc_sum[...] = jnp.zeros_like(acc_sum)
     acc_hit[...] = jnp.zeros_like(acc_hit)
     zbuf[...] = jnp.zeros_like(zbuf)
     stats[...] = jnp.zeros_like(stats)
+    setup()
+    project()
+    attend(0)
     pl.semaphore_wait(barrier, 3)
-    part_copy.wait()
 
     split = FIRST_GROUPS
     groups = tiles // GROUP
     total_tiles = tiles + split * GROUP
     scatter_start(0, 0)
+    attend(1)
+    for copy in weight_loads()[5:15]:
+        copy.start(priority=1)
     scatter_forward(0, 0)
     scatter_finish_gather_start(0, 0)
     gather_forward(0, 1)
@@ -362,7 +417,7 @@
     for c in range(CHUNKS):
         for k in range(2):
             lo = (c * 2 + k) * rows
-            logprob_ref[:, k * half + c * rows:k * half + (c + 1) * rows] = result[:, lo:lo + rows]
+            logprob_ref[k * half + c * rows:k * half + (c + 1) * rows] = result[:, lo:lo + rows].reshape(rows)
 
     for copy in y_copies(CHUNKS - 1):
         copy.wait()
@@ -373,7 +428,7 @@
         pair_copy(c).wait_send()
 
 
-def layer_head(part, x, target, g_attn_post, g_mlp_pre, g_mlp_post, g_final, w_gate, w_up, w_down, table):
+def layer_head(x, lens, target, g_attn_pre, w_q, w_k, w_v, w_o, g_attn_post, g_mlp_pre, w_gate, w_up, w_down, g_mlp_post, g_final, k_cache, v_cache, table):
     tokens, width = x.shape
     half = tokens // 2
     rows = half // CHUNKS
@@ -381,13 +436,14 @@
     vmem, dma = pltpu.VMEM, pltpu.SemaphoreType.DMA
     any_spec = pl.BlockSpec(memory_space=pl.ANY)
     vmem_spec = pl.BlockSpec(memory_space=pltpu.VMEM)
-    gains = [g.astype(f32)[None, :] for g in (g_attn_post, g_mlp_pre, g_mlp_post, g_final)]
-    ordered = target.reshape(2, CHUNKS, rows).transpose(1, 0, 2).reshape(1, tokens)
-    logprob, hidden = pl.pallas_call(
+    freq = (ROPE_BASE ** (-2.0 * np.arange(HEAD_DIM // 2) / HEAD_DIM)).astype(np.float32)[None, :]
+    k_rows = k_cache.reshape(tokens * CONTEXT, HEAD_DIM)
+    v_rows = v_cache.reshape(tokens * CONTEXT, HEAD_DIM)
+    return pl.pallas_call(
         layer_head_kernel,
-        in_specs=[any_spec, any_spec] + [vmem_spec] * 5 + [any_spec] * 4,
+        in_specs=[vmem_spec] * 8 + [any_spec] * 11,
         out_specs=[vmem_spec, any_spec],
-        out_shape=[jax.ShapeDtypeStruct((1, tokens), f32), jax.ShapeDtypeStruct((tokens, width), bf16)],
+        out_shape=[jax.ShapeDtypeStruct((tokens,), f32), jax.ShapeDtypeStruct((tokens, width), bf16)],
         scratch_shapes=[
             vmem((SLOTS * TILE, width), bf16),
             vmem((half, width), f32),
@@ -396,18 +452,20 @@
             vmem((half, width), f32),
             vmem((tokens, width), bf16),
             vmem((half, width), bf16),
-            vmem((rows, width), bf16),
-            vmem((rows, width), bf16),
+            vmem((2 * rows, width), bf16),
             vmem((2 * CHUNKS, BLOCK, width), bf16),
-            vmem((2 * CHUNKS, BLOCK, width), bf16),
+            vmem((half, 4 * HEAD_DIM), f32),
+            vmem((2, half, HEAD_DIM // 2), f32),
+            vmem((half, rows), f32),
+            vmem((8, width), f32),
+            vmem((1, tokens), jnp.int32),
             vmem((SUB, tokens), f32),
             vmem((8, tokens), f32),
             vmem((8, tokens), f32),
             vmem((3, 8, tokens), f32),
             vmem((3, 8, tokens), f32),
             dma((SLOTS,)),
-            dma,
-            dma((2 * CHUNKS,)),
+            dma((13,)),
             dma((CHUNKS, 2)),
             dma((4, CHUNKS, 6)),
             dma((4, CHUNKS, 6)),
@@ -418,25 +476,9 @@
         ],
         compiler_params=pltpu.CompilerParams(collective_id=0, has_side_effects=True, vmem_limit_bytes=66_500_000),
         name='layer_head',
-    )(part, x, ordered, *gains, w_gate, w_up, w_down, table)
-    return logprob.reshape(tokens), hidden
+    )(lens, target, freq, g_attn_pre, g_attn_post, g_mlp_pre, g_mlp_post, g_final, x, w_q, w_k, w_v, w_o, k_rows, v_rows, w_gate, w_up, w_down, table)
 
 
 def solution(mesh):
     in_specs = (P(), P(), P(), P(), P(None, 't'), P(None, 't'), P(None, 't'), P('t', None), P(), P(), P(None, 't'), P(None, 't'), P('t', None), P(), P(), P(None, None, 't', None), P(None, None, 't', None), P(('v', 't'), None))
-
-    def local_step(hidden_in, seq_lens, target, g_attn_pre, w_q, w_k, w_v, w_o, g_attn_post, g_mlp_pre, w_gate, w_up, w_down, g_mlp_post, g_final, k_cache, v_cache, embed_table):
-        half = hidden_in.shape[0] // 2
-        first = lax.axis_index('v') * half
-
-        def mine(array):
-            return lax.dynamic_slice_in_dim(array, first, half, 0)
-
-        lens = mine(seq_lens)
-        normed = rms_norm(mine(hidden_in), g_attn_pre).astype(jnp.bfloat16)
-        attn_vec = attention(normed, lens, w_q, w_k, w_v, mine(k_cache), mine(v_cache))
-        part = jnp.dot(attn_vec, w_o, preferred_element_type=jnp.float32)
-        logprob, hidden_out = layer_head(part, hidden_in, target, g_attn_post, g_mlp_pre, g_mlp_post, g_final, w_gate, w_up, w_down, embed_table)
-        return logprob, hidden_out
-
-    return jax.shard_map(local_step, mesh=mesh, in_specs=in_specs, out_specs=(P(), P()), check_vma=False)
+    return jax.shard_map(layer_head, mesh=mesh, in_specs=in_specs, out_specs=(P(), P()), check_vma=False)

time: 239 us -> 206 us (0.86)
  matrix products: 15.4 us -> 0 us
  other arithmetic: 7.96 us -> 0 us
  local copies, waits for them, and re-layouts: 12.3 us -> 4.65 us
    dot_general x6 -> x0, matrix products: 15.4 us -> none  [the longest x1 3.52 us: attention(): jnp.einsum('nkgd,ntkd->nkgt', q_rot, k_cache, preferred_element_type=jnp....]
    broadcast_in_dim x4 -> x0, local copies, waits for them, and re-layouts: 5.17 us -> none  [layer_head(): g.astype(f32)[None, :]]
    unnamed x14 -> x2, local copies, waits for them, and re-layouts: 4.85 us -> 4.65 us
where the time goes in v3:
time: 206 us
  Pallas kernels  200 us (97%)
  local copies, waits for them, and re-layouts  4.65 us (2%)
    pallas_call x1, Pallas kernels, layer_head(): pl.pallas_call(layer_head_kernel, in_specs=[vmem_spec] * 8 + [any_spec] *...  200 us
    unnamed x2, local copies, waits for them, and re-layouts  4.65 us

profile of v3, /device:TPU:0, one launch (start us, length us, event | category | flops | bytes accessed | tf_op | source)
XLA Modules:
  0.0 205.7 jit_solution(5674679435282913997)
XLA Ops:
  0.6 200.4 %layer_head.1 = (f32[512]{0:T(512)}, bf16[512,2560]{1,0:T(8,128)(2,1)}) custom-call(s32[512]{0:T(512)} %lens_in.1, s32[512]{0:T(512)} %tgt_in.1, f32[1,128]{1,0:T(1,128)} %constant.2.clone.freq_ref, bf16[2560]{0:T(1024)(128)(2,1)} %g_first_in.1, bf16[2560]{0:T(1024)(128)(2,1)} %g_attn_in.1, bf16[2560]{0:T(1024)(128)(2,1)} %g_pre_in.1, ...), custom_call_target="tpu_custom_call" | custom-call | tf_op jit(solution)/shard_map/layer_head/pallas_call | solution.py:442
  201.1 1.2 copy.23
  202.3 3.4 %copy.24 = bf16[512,2560]{1,0:T(8,128)(2,1)} copy(bf16[512,2560]{1,0:T(8,128)(2,1)} %get-tuple-element.5) | data formatting | bytes 5242880
